TPU v7x, 32 devices: a whole 2x2x4 slice. The times are simulated.
32 devices in a mesh: row: 8 (over y, x, core), col: 4 (over z).
Axes of the slice: x: 2, y: 2, z: 4, core: 2. Of those that a mesh axis runs over, the one named last changes fastest.
Arguments:
- velocity: float32 [128, 128, 2048], P(None, 'row', 'col'), may hold values from -6 to 6
- symbol_x: float32 [128], replicated, may hold values from 0.3 to 3
- symbol_y: float32 [128], replicated, may hold values from 0.3 to 3
- symbol_z: float32 [2048], replicated, may hold values from 0.3 to 3
Outputs:
- coefficients: float32 [128, 128, 2048], P('row', 'col')
All inputs are finite; a program needn't handle non-finite values.
Results may differ from a plain program's by a relative error of at most 0.000076.
Values sent between devices are 32-bit elements; how exact they have to be, the bound alone decides.
A program may use at most 192 MiB of HBM per device.

v0:
```python
import jax
import jax.numpy as jnp
from jax import lax
from jax.sharding import PartitionSpec as P


def mode_table(count):
    rank = jnp.arange(count)
    angle = 2.0 * jnp.pi / count * (rank[:, None] * rank[None, :] % count).astype(jnp.float32)
    return (jnp.cos(angle) + jnp.sin(angle)) * count ** (-0.5)


def along_dim(values, dim):
    moved = jnp.tensordot(
        values, mode_table(values.shape[dim]), axes=([dim], [0]), precision=lax.Precision.HIGHEST
    )
    return jnp.moveaxis(moved, -1, dim)


def local(velocity, symbol_x, symbol_y, symbol_z):
    part_values = velocity
    part_values = along_dim(part_values, 0)
    part_values = lax.all_to_all(part_values, "row", split_axis=0, concat_axis=1, tiled=True)
    part_values = along_dim(part_values, 1)
    pencil_values = part_values
    pencil_values = lax.all_to_all(pencil_values, "col", split_axis=1, concat_axis=2, tiled=True)
    pencil_values = along_dim(pencil_values, 2)
    share_x = pencil_values.shape[0]
    part_x = lax.dynamic_slice_in_dim(symbol_x, lax.axis_index("row") * share_x, share_x)
    share_y = pencil_values.shape[1]
    part_y = lax.dynamic_slice_in_dim(symbol_y, lax.axis_index("col") * share_y, share_y)
    symbol = part_x[:, None, None] + part_y[None, :, None] + symbol_z[None, None, :]
    pencil_values = pencil_values * ((1.0 - 0.2 * symbol) / (1.0 + 0.2 * symbol))
    return pencil_values


def solution(mesh):
    placed = (P(None, "row", "col"), P(), P(), P())
    return jax.shard_map(
        local, mesh=mesh, in_specs=placed, out_specs=P("row", "col", None), check_vma=False
    )
```

profile of v0, /device:TPU:0, one launch (start us, length us, event | category | flops | bytes accessed | tf_op | source)
XLA Modules:
  0.0 224.9 jit_solution(18273751174371291723)
XLA Ops:
  0.0 9.0 %fusion.19 = f32[128,16,512]{2,0,1:T(8,128)S(1)} fusion(f32[128,16,512]{2,1,0:T(8,128)} %param.4), kind=kOutput, calls=%fused_computation.20 | convolution fusion | flops 1610874880 | bytes 8388608 | tf_op jit(solution)/shard_map/dot_general | solution.py:14
  9.0 2.4 %copy.24 = f32[128,16,512]{2,1,0:T(8,128)S(1)} copy(f32[128,16,512]{2,0,1:T(8,128)S(1)} %fusion.19) | data formatting | bytes 8388608 | tf_op jit(solution)/shard_map/dot_general | solution.py:14
  11.5 54.0 %all_to_all.36 = f32[128,16,512]{2,1,0:T(8,128)S(1)} all-to-all(f32[128,16,512]{2,1,0:T(8,128)S(1)} %copy.24), channel_id=1, replica_groups=mesh['row'=8,'col'=4] {'row'}, dimensions={0} | all-to-all | bytes 8388608 | tf_op jit(solution)/shard_map/all_to_all | solution.py:23
  65.5 0.8 copy.25
  66.3 8.6 %convolution_bitcast_fusion = f32[16,128,512]{1,2,0:T(8,128)} fusion(f32[16,128,512]{2,1,0:T(8,128)S(1)} %bitcast.28), kind=kOutput, calls=%fused_computation.23 | convolution fusion | flops 1610874880 | bytes 8388608 | tf_op jit(solution)/shard_map/dot_general | solution.py:14
  75.0 5.5 %copy.27 = f32[16,128,512]{2,0,1:T(8,128)} copy(f32[16,128,512]{1,2,0:T(8,128)} %convolution_bitcast_fusion) | data formatting | bytes 8388608 | tf_op jit(solution)/shard_map/transpose | solution.py:17
  80.5 0.0 copy-start.1
  80.5 0.0 copy-start.2
  80.5 5.1 %all-to-all-start.1 = ((f32[16,128,512]{2,0,1:T(8,128)}), f32[16,128,512]{2,0,1:T(8,128)}, u32[]{:S(2)}, u32[]{:S(2)}) async-start(f32[16,128,512]{2,0,1:T(8,128)} %copy.27), calls=%async_computation.1 | async-start | bytes 8388608 | tf_op jit(solution)/shard_map/all_to_all | solution.py:26
  85.6 0.0 copy-done.1
  85.6 0.1 dynamic_slice.7
  85.7 0.0 copy-done.2
  85.7 0.1 dynamic_slice.6
  85.8 0.1 broadcast_add_fusion
  85.9 67.7 %fusion.51 = f32[2048,2048,1]{1,0,2:T(8,128)} fusion(), kind=kLoop, calls=%fused_computation.7.clone.clone.clone.1 | loop fusion | flops 67108864 | bytes 16777216 | tf_op jit(solution)/shard_map/dot_general | solution.py:14
  153.5 25.0 %all-to-all-done.1 = f32[16,128,512]{2,0,1:T(8,128)} async-done(((f32[16,128,512]{2,0,1:T(8,128)}), f32[16,128,512]{2,0,1:T(8,128)}, u32[]{:S(2)}, u32[]{:S(2)}) %all-to-all-start.1) | async-done | bytes 4194336 | tf_op jit(solution)/shard_map/all_to_all | solution.py:26
  178.5 6.9 %copy.29 = f32[16,32,4,512]{3,2,1,0:T(4,128)} copy(f32[16,32,4,512]{3,0,1,2:T(8,128)} %bitcast.8) | data formatting | bytes 8388608 | tf_op jit(solution)/shard_map/all_to_all | solution.py:26
  185.4 0.0 copy-start
  185.4 6.1 %all_to_all.33 = f32[16,32,2048]{2,1,0:T(8,128)} reshape(f32[16,32,4,512]{3,2,1,0:T(4,128)} %copy.29) | data formatting | bytes 8388608 | tf_op jit(solution)/shard_map/all_to_all | solution.py:26
  191.5 0.0 copy-done
  191.5 33.4 %divide_multiply_fusion = f32[16,32,2048]{2,1,0:T(8,128)} fusion(f32[16,32,2048]{2,1,0:T(8,128)} %all_to_all.33, f32[2048]{0:T(1024)S(1)} %copy-done, f32[16,32]{1,0:T(8,128)S(1)} %broadcast_add_fusion, f32[2048,2048,1]{1,0,2:T(8,128)} %fusion.51), kind=kOutput, calls=%fused_computation.22 | convolution fusion | flops 25776095232 | bytes 25176064 | tf_op jit(solution)/shard_map/dot_general | solution.py:14
Async XLA Ops:
  80.5 5.2 %copy-start.1 = (f32[128]{0:T(128)S(1)}, f32[128]{0:T(128)}, u32[]{:S(2)}) copy-start(f32[128]{0:T(128)} %param.6) | copy-start | bytes 1540
  80.5 5.3 %copy-start.2 = (f32[128]{0:T(128)S(1)}, f32[128]{0:T(128)}, u32[]{:S(2)}) copy-start(f32[128]{0:T(128)} %param.5) | copy-start | bytes 1540
  80.5 98.1 %all-to-all-start.1 = ((f32[16,128,512]{2,0,1:T(8,128)}), f32[16,128,512]{2,0,1:T(8,128)}, u32[]{:S(2)}, u32[]{:S(2)}) async-start(f32[16,128,512]{2,0,1:T(8,128)} %copy.27), calls=%async_computation.1 | async-start | bytes 8388608 | tf_op jit(solution)/shard_map/all_to_all | solution.py:26
  185.4 6.1 %copy-start = (f32[2048]{0:T(1024)S(1)}, f32[2048]{0:T(1024)}, u32[]{:S(2)}) copy-start(f32[2048]{0:T(1024)} %param.7) | copy-start | bytes 24580
where the time goes:
time: 225 us
  other arithmetic  67.8 us (30%)
  blocking collectives  54 us (24%)
  matrix products  51 us (23%)
  waiting for transfers between devices  25 us (11%)
  local copies, waits for them, and re-layouts  21.9 us (10%)
  starting transfers between devices  5.15 us (2%)
    dot_general x1, other arithmetic, along_dim(): jnp.tensordot(values, mode_table(values.shape[dim]), axes=([dim], [0]), p...  67.7 us
    all_to_all x1, blocking collectives, local(): lax.all_to_all(part_values, 'row', split_axis=0, concat_axis=1, tiled=True)  54 us
    dot_general x3, matrix products, along_dim(): jnp.tensordot(values, mode_table(values.shape[dim]), axes=([dim], [0]), p...  51 us
    all_to_all x1, waiting for transfers between devices, local(): lax.all_to_all(pencil_values, 'col', split_axis=1, concat_axis=2, tiled=T...  25 us
    all_to_all x2, local copies, waits for them, and re-layouts, local(): lax.all_to_all(pencil_values, 'col', split_axis=1, concat_axis=2, tiled=T...  13 us
    transpose x1, local copies, waits for them, and re-layouts, along_dim(): return jnp.moveaxis(moved, -1, dim)  5.51 us
    all_to_all x1, starting transfers between devices, local(): lax.all_to_all(pencil_values, 'col', split_axis=1, concat_axis=2, tiled=T...  5.15 us
  transfers between devices with their start and end apart: 1, of which 1 were waited for; matrix products, arithmetic and copies ran while one was open for 30% of the time, Pallas kernels for 0%

commit v1 on v0

--- a/solution.py
+++ b/solution.py
@@ -23,7 +23,12 @@
     part_values = lax.all_to_all(part_values, "row", split_axis=0, concat_axis=1, tiled=True)
     part_values = along_dim(part_values, 1)
     pencil_values = part_values
-    pencil_values = lax.all_to_all(pencil_values, "col", split_axis=1, concat_axis=2, tiled=True)
+    pencil_values = jnp.concatenate(
+        lax.all_to_all(
+            jnp.stack(jnp.split(pencil_values, lax.axis_size("col"), axis=1)), "col", 0, 0
+        ),
+        axis=2,
+    )
     pencil_values = along_dim(pencil_values, 2)
     share_x = pencil_values.shape[0]
     part_x = lax.dynamic_slice_in_dim(symbol_x, lax.axis_index("row") * share_x, share_x)

time: 225 us -> 206 us (0.916)
  local copies, waits for them, and re-layouts: 21.9 us -> 6.86 us
  matrix products: 51 us -> 44.3 us
  other arithmetic: 67.8 us -> 70.3 us
    all_to_all x2 -> x0, local copies, waits for them, and re-layouts: 13 us -> none  [local(): lax.all_to_all(pencil_values, 'col', split_axis=1, concat_axis=2, tiled=T...]
    dot_general x3, matrix products: 51 us -> 44.3 us  [along_dim(): jnp.tensordot(values, mode_table(values.shape[dim]), axes=([dim], [0]), p...]
    transpose x1 -> x0, local copies, waits for them, and re-layouts: 5.51 us -> none  [along_dim(): return jnp.moveaxis(moved, -1, dim)]
    reshape x0 -> x1, local copies, waits for them, and re-layouts: none -> 2.64 us  [local(): jnp.concatenate(lax.all_to_all(jnp.stack(jnp.split(pencil_values, lax.axi...]
    another operation x0 -> x1, other arithmetic: none -> 2.52 us  [local(): jnp.stack(jnp.split(pencil_values, lax.axis_size('col'), axis=1))]
  transfers between devices with their start and end apart: 1 -> 1, of which waited for: 1 -> 1; matrix products, arithmetic and copies ran while one was open for 30% -> 33% of each run, Pallas kernels for 0% -> 0%
where the time goes in v1:
time: 206 us
  other arithmetic  70.3 us (34%)
  blocking collectives  54 us (26%)
  matrix products  44.3 us (22%)
  waiting for transfers between devices  25 us (12%)
  local copies, waits for them, and re-layouts  6.86 us (3%)
  starting transfers between devices  5.2 us (3%)
    dot_general x1, other arithmetic, along_dim(): jnp.tensordot(values, mode_table(values.shape[dim]), axes=([dim], [0]), p...  67.7 us
    all_to_all x1, blocking collectives, local(): lax.all_to_all(part_values, 'row', split_axis=0, concat_axis=1, tiled=True)  54 us
    dot_general x3, matrix products, along_dim(): jnp.tensordot(values, mode_table(values.shape[dim]), axes=([dim], [0]), p...  44.3 us
    all_to_all x1, waiting for transfers between devices, local(): lax.all_to_all(jnp.stack(jnp.split(pencil_values, lax.axis_size('col'), a...  25 us
    all_to_all x1, starting transfers between devices, local(): lax.all_to_all(jnp.stack(jnp.split(pencil_values, lax.axis_size('col'), a...  5.2 us
  transfers between devices with their start and end apart: 1, of which 1 were waited for; matrix products, arithmetic and copies ran while one was open for 33% of the time, Pallas kernels for 0%

profile of v1, /device:TPU:0, one launch (start us, length us, event | category | flops | bytes accessed | tf_op | source)
XLA Modules:
  0.0 205.7 jit_solution(4706164993764963773)
XLA Ops:
  0.0 8.4 %fusion.19 = f32[128,16,512]{2,0,1:T(8,128)S(1)} fusion(f32[128,16,512]{2,1,0:T(8,128)} %param.4), kind=kOutput, calls=%fused_computation.21 | convolution fusion | flops 1610874880 | bytes 8388608 | tf_op jit(solution)/shard_map/dot_general | solution.py:14
  8.5 2.4 %copy.11 = f32[128,16,512]{2,1,0:T(8,128)S(1)} copy(f32[128,16,512]{2,0,1:T(8,128)S(1)} %fusion.19) | data formatting | bytes 8388608 | tf_op jit(solution)/shard_map/dot_general | solution.py:14
  10.9 54.0 %all_to_all.23 = f32[128,16,512]{2,1,0:T(8,128)S(1)} all-to-all(f32[128,16,512]{2,1,0:T(8,128)S(1)} %copy.11), channel_id=1, replica_groups=mesh['row'=8,'col'=4] {'row'}, dimensions={0} | all-to-all | bytes 8388608 | tf_op jit(solution)/shard_map/all_to_all | solution.py:23
  64.9 0.8 copy.12
  65.8 4.7 %convolution_bitcast_fusion = f32[16,128,512]{2,1,0:T(8,128)S(1)} fusion(f32[16,128,512]{2,1,0:T(8,128)S(1)} %bitcast.35), kind=kOutput, calls=%fused_computation.24 | convolution fusion | flops 1610874880 | bytes 8388608 | tf_op jit(solution)/shard_map/dot_general | solution.py:14
  70.5 0.8 slice_bitcast_fusion.3
  71.3 2.5 %pad_maximum_fusion = f32[4,16,32,512]{3,2,1,0:T(8,128)} fusion(f32[1,16,32,512]{3,2,1,0:T(8,128)S(1)} %get-tuple-element.6, f32[1,16,32,512]{3,2,1,0:T(8,128)S(1)} %get-tuple-element.7, f32[1,16,32,512]{3,2,1,0:T(8,128)S(1)} %get-tuple-element.8, f32[1,16,32,512]{3,2,1,0:T(8,128)S(1)} %get-tuple-element.5), kind=kLoop, calls=%fused_computation.20 | loop fusion | flops 3145728 | bytes 8388608 | tf_op jit(solution)/shard_map/stack | solution.py:28
  73.8 0.0 copy-start.1
  73.8 0.0 copy-start.2
  73.8 5.2 %all-to-all-start.1 = ((f32[4,16,32,512]{3,2,1,0:T(8,128)}), f32[4,16,32,512]{3,2,1,0:T(8,128)}, u32[]{:S(2)}, u32[]{:S(2)}) async-start(f32[4,16,32,512]{3,2,1,0:T(8,128)} %pad_maximum_fusion), calls=%async_computation.1 | async-start | bytes 8388608 | tf_op jit(solution)/shard_map/all_to_all | solution.py:27
  79.0 0.0 copy-done.1
  79.1 0.1 dynamic_slice.7
  79.1 0.0 copy-done.2
  79.1 0.1 dynamic_slice.6
  79.2 0.1 broadcast_add_fusion
  79.3 67.7 %fusion.51 = f32[2048,2048,1]{1,0,2:T(8,128)} fusion(), kind=kLoop, calls=%fused_computation.7.clone.clone.clone.1 | loop fusion | flops 67108864 | bytes 16777216 | tf_op jit(solution)/shard_map/dot_general | solution.py:14
  147.0 25.0 %all-to-all-done.1 = f32[4,16,32,512]{3,2,1,0:T(8,128)} async-done(((f32[4,16,32,512]{3,2,1,0:T(8,128)}), f32[4,16,32,512]{3,2,1,0:T(8,128)}, u32[]{:S(2)}, u32[]{:S(2)}) %all-to-all-start.1) | async-done | bytes 4194336 | tf_op jit(solution)/shard_map/all_to_all | solution.py:27
  171.9 0.0 copy-start
  171.9 2.6 %copy.14 = f32[4,16,4,8,512]{4,3,0,2,1:T(8,128)S(1)} copy(f32[4,16,4,8,512]{4,3,2,1,0:T(8,128)} %bitcast.12) | data formatting | bytes 8388608 | tf_op jit(solution)/shard_map/reshape | solution.py:26
  174.6 0.0 copy-done
  174.6 31.1 %divide_multiply_fusion = f32[16,32,2048]{2,1,0:T(8,128)} fusion(f32[16,32,2048]{2,1,0:T(8,128)S(1)} %bitcast.36, f32[2048]{0:T(1024)S(1)} %copy-done, f32[16,32]{1,0:T(8,128)S(1)} %broadcast_add_fusion, f32[2048,2048,1]{1,0,2:T(8,128)} %fusion.51), kind=kOutput, calls=%fused_computation.23 | convolution fusion | flops 25776095232 | bytes 25176064 | tf_op jit(solution)/shard_map/dot_general | solution.py:14
Async XLA Ops:
  73.8 5.2 %copy-start.1 = (f32[128]{0:T(128)S(1)}, f32[128]{0:T(128)}, u32[]{:S(2)}) copy-start(f32[128]{0:T(128)} %param.6) | copy-start | bytes 1540
  73.8 5.3 %copy-start.2 = (f32[128]{0:T(128)S(1)}, f32[128]{0:T(128)}, u32[]{:S(2)}) copy-start(f32[128]{0:T(128)} %param.5) | copy-start | bytes 1540
  73.8 98.1 %all-to-all-start.1 = ((f32[4,16,32,512]{3,2,1,0:T(8,128)}), f32[4,16,32,512]{3,2,1,0:T(8,128)}, u32[]{:S(2)}, u32[]{:S(2)}) async-start(f32[4,16,32,512]{3,2,1,0:T(8,128)} %pad_maximum_fusion), calls=%async_computation.1 | async-start | bytes 8388608 | tf_op jit(solution)/shard_map/all_to_all | solution.py:27
  171.9 2.6 %copy-start = (f32[2048]{0:T(1024)S(1)}, f32[2048]{0:T(1024)}, u32[]{:S(2)}) copy-start(f32[2048]{0:T(1024)} %param.7) | copy-start | bytes 24580
